TPU v7x, 32 devices: a whole 2x2x4 slice. The times are simulated.
32 devices in a mesh: grp: 2 (over y), blk: 8 (over z, x), uly: 2 (over core).
Axes of the slice: x: 2, y: 2, z: 4, core: 2. Of those that a mesh axis runs over, the one named last changes fastest.
Arguments:
- query: bfloat16 [512, 1152], P(('grp', 'blk', 'uly')), parts along dimension 0, may hold values from -6 to 6
- key: bfloat16 [512, 1152], P(('grp', 'blk', 'uly')), parts along dimension 0, may hold values from -6 to 6
- value: bfloat16 [512, 1152], P(('grp', 'blk', 'uly')), parts along dimension 0, may hold values from -6 to 6
- q_gain: float32 [96], replicated, may hold values from 1 to 2.5
- k_gain: float32 [96], replicated, may hold values from 1 to 2.5
- out_weight: bfloat16 [1152, 2304], P('uly'), may hold values from -0.1875 to 0.1875
Outputs:
- mixed: bfloat16 [512, 2304], P(('grp', 'blk', 'uly')), parts along dimension 0
There are 2 independent parts, one for each index of `grp`. A program takes and returns all parts, laid end to end along the dimension named above; an argument that names none is the same for every part. Nothing has to cross between parts.
All inputs are finite; a program needn't handle non-finite values.
Results may differ from a plain program's by a relative error of at most 0.012.
Values may be sent and summed in bfloat16 or wider, within the bound.
A program may use at most 128 MiB of HBM per device.

v0:
```python
import functools

import jax
import jax.numpy as jnp
from jax import lax
from jax.experimental import pallas as pl
from jax.experimental.pallas import tpu as pltpu
from jax.sharding import PartitionSpec as P

HD = 96
LANES = 128
CHUNKS = 1
GROUPS = 4
MESH = pl.DeviceIdType.MESH


def loop(count, body):
    if count <= 32:
        for i in range(count):
            body(i)
    else:
        lax.fori_loop(0, count, lambda i, c: (body(i), c)[1], 0)


def take(ref, sem):
    pltpu.make_async_copy(ref, ref, sem).wait()


def layer_kernel(
    blks, ulys, heads, copies,
    q_hbm, k_hbm, v_hbm, qg_hbm, kg_hbm, w_hbm, out_ref,
    raw, gains, w_vmem, pack, qkv, attn, back, acc,
    load_sem, gain_sem, w_sem, send1, recv1, send2, recv2, send_w, recv_w,
):
    n = blks * ulys
    rows = raw.shape[1]
    owners = heads * copies
    blk, uly = lax.axis_index("blk"), lax.axis_index("uly")
    me = blk * ulys + uly
    seq = n * rows
    block = seq // copies
    chunks = CHUNKS
    chunk = block // chunks
    groups = recv2.shape[0]
    members = heads // groups
    targets = chunk // rows
    depth = w_hbm.shape[0]
    upper = (2 * me) // n

    barrier = pltpu.get_barrier_semaphore()

    def greet(i):
        d = lax.rem(me + n // 2 + i + i // (n // 2), n)
        pl.semaphore_signal(
            barrier, inc=1, device_id={"blk": d // ulys, "uly": d % ulys}, device_id_type=MESH
        )

    loop(n - 1, greet)

    loads = [
        pltpu.make_async_copy(src, raw.at[i], load_sem.at[i])
        for i, src in enumerate((q_hbm, k_hbm, v_hbm))
    ]
    load_gains = [
        pltpu.make_async_copy(src, gains.at[i], gain_sem)
        for i, src in enumerate((qg_hbm, kg_hbm))
    ]
    for one in loads + load_gains:
        one.start()

    def mirror(d):
        plane = d // 4
        return d + (plane % 2) * (3 - 2 * (d % 4))

    def owner_device(o):
        return mirror(o * n // owners)

    spot = mirror(me)
    slot = (spot * owners + n - 1) // n
    is_owner = jnp.logical_and(slot < owners, (slot * n) // owners == spot)
    slot = jnp.minimum(slot, owners - 1)

    my_depth = pl.ds(pl.multiple_of(uly * depth, depth), depth)
    load_w = pltpu.make_async_copy(w_hbm, w_vmem.at[my_depth], w_sem)
    load_w.start()

    pad = jnp.zeros((rows, LANES - HD), jnp.bfloat16)
    take(gains, gain_sem)
    for i in range(2):
        loads[i].wait()
        gain = gains[i]
        for h in range(heads):
            x = raw[i, :, h * HD:(h + 1) * HD].astype(jnp.float32)
            scale = lax.rsqrt(jnp.mean(x * x, axis=-1, keepdims=True) + 1e-06)
            normed = (x * scale * gain).astype(jnp.bfloat16)
            pack[h, :, i * LANES:(i + 1) * LANES] = jnp.concatenate([normed, pad], axis=1)
    loads[2].wait()
    for h in range(heads):
        x = raw[2, :, h * HD:(h + 1) * HD]
        pack[h, :, 2 * LANES:3 * LANES] = jnp.concatenate([x, pad], axis=1)

    pl.semaphore_wait(barrier, n - 1)

    my_rows = pl.ds(pl.multiple_of(me * rows, rows), rows)

    def send_of(o):
        d = owner_device(o)
        return d, pltpu.make_async_remote_copy(
            src_ref=pack.at[o // copies],
            dst_ref=qkv.at[my_rows],
            send_sem=send1,
            recv_sem=recv1,
            device_id={"blk": d // ulys, "uly": d % ulys},
            device_id_type=MESH,
        )

    def send(i):
        d, copy = send_of(owners - 1 - i + upper * (2 * i + 1 - owners))

        @pl.when(d != me)
        def _():
            copy.start()

    loop(owners, send)

    give_w = pltpu.make_async_remote_copy(
        src_ref=w_hbm,
        dst_ref=w_vmem.at[my_depth],
        send_sem=send_w,
        recv_sem=recv_w,
        device_id={"blk": blk, "uly": 1 - uly},
        device_id_type=MESH,
    )
    give_w.start()

    @pl.when(is_owner)
    def _():
        head = slot // copies
        part = slot % copies
        qkv[my_rows, :] = pack[head]

        take(qkv.at[pl.ds(0, (n - 1) * rows)], recv1)
        score_scale = float(HD) ** (-0.5)

        def step(query, j, carry):
            weighted, total = carry
            here = pl.ds(j * block, block)
            keys = qkv[here, LANES:2 * LANES]
            values = qkv[here, 2 * LANES:3 * LANES]
            scores = lax.dot_general(
                query, keys, (((1,), (1,)), ((), ())), preferred_element_type=jnp.float32
            ) * score_scale
            expd = jnp.exp(scores)
            total = total + jnp.sum(expd, axis=-1, keepdims=True)
            weighted = weighted + jnp.dot(
                expd.astype(jnp.bfloat16), values, preferred_element_type=jnp.float32
            )
            return weighted, total

        def result_copies(c):
            for k in range(targets):
                i = targets - 1 - k + upper * (2 * k + 1 - targets)
                d = (part * chunks + c) * targets + i
                src = attn.at[pl.ds(pl.multiple_of((c * targets + i) * rows, rows), rows)]
                yield (
                    d == me,
                    functools.partial(
                        pltpu.make_async_copy, src, back.at[head], recv2.at[head // members]
                    ),
                    pltpu.make_async_remote_copy(
                        src_ref=src,
                        dst_ref=back.at[head],
                        send_sem=send2,
                        recv_sem=recv2.at[head // members],
                        device_id={"blk": d // ulys, "uly": d % ulys},
                        device_id_type=MESH,
                    ),
                )

        for k in range(chunks):
            c = chunks - 1 - k + upper * (2 * k + 1 - chunks)
            at = part * block + c * chunk
            query = qkv[pl.ds(pl.multiple_of(at, chunk), chunk), 0:LANES]
            carry = (jnp.zeros((chunk, LANES), jnp.float32), jnp.zeros((chunk, 1), jnp.float32))
            if copies == 1:
                weighted, total = step(query, 0, carry)
            else:
                weighted, total = lax.fori_loop(
                    0, copies, functools.partial(lambda q, j, c: step(q, j, c), query), carry
                )
            attn[pl.ds(pl.multiple_of(c * chunk, chunk), chunk), :] = (weighted / total).astype(jnp.bfloat16)
            for home, local, remote in result_copies(c):
                pl.when(home)(lambda local=local: local().start())
                pl.when(jnp.logical_not(home))(remote.start)

    load_w.wait()
    give_w.wait_recv()
    first = (me * groups) // n
    for i in range(groups):
        g = lax.rem(first + i * (1 - 2 * upper) + groups, groups)
        take(back.at[pl.ds(g * members, members)], recv2.at[g])
        for j in range(members):
            h = g * members + j
            term = jnp.dot(
                back[h, :, 0:HD],
                w_vmem[pl.ds(pl.multiple_of(h * HD, HD), HD), :],
                preferred_element_type=jnp.float32,
            )
            if i == 0 and j == 0:
                acc[...] = term
            elif i < groups - 1 or j < members - 1:
                acc[...] += term
            else:
                out_ref[...] = (acc[...] + term).astype(out_ref.dtype)

    give_w.wait_send()
    for i in range(copies - 1):
        take(pack, send1)

    @pl.when(is_owner)
    def _():
        take(pack.at[pl.ds(0, heads - 1)], send1)
        at_home = (slot % copies) * block == (me * rows) // block * block
        pl.when(at_home)(lambda: take(attn.at[pl.ds(0, block - rows)], send2))
        pl.when(jnp.logical_not(at_home))(lambda: take(attn, send2))

    @pl.when(jnp.logical_not(is_owner))
    def _():
        take(pack, send1)


def on_device(blks, ulys, query, key, value, q_gain, k_gain, out_weight):
    rows, width = query.shape
    heads = width // HD
    n = blks * ulys
    copies = 1
    while heads * copies * 2 <= n:
        copies *= 2
    owners = heads * copies
    depth, cols = out_weight.shape
    seq = n * rows
    block = seq // copies
    dma = pltpu.SemaphoreType.DMA
    return pl.pallas_call(
        functools.partial(layer_kernel, blks, ulys, heads, copies),
        out_shape=pltpu.VMEM((rows, cols), jnp.bfloat16),
        in_specs=[pl.BlockSpec(memory_space=pltpu.HBM)] * 6,
        out_specs=pl.BlockSpec(memory_space=pltpu.VMEM),
        scratch_shapes=[
            pltpu.VMEM((3, rows, width), jnp.bfloat16),
            pltpu.VMEM((2, 1, HD), jnp.float32),
            pltpu.VMEM((width, cols), jnp.bfloat16),
            pltpu.VMEM((heads, rows, 3 * LANES), jnp.bfloat16),
            pltpu.VMEM((seq, 3 * LANES), jnp.bfloat16),
            pltpu.VMEM((block, LANES), jnp.bfloat16),
            pltpu.VMEM((heads, rows, LANES), jnp.bfloat16),
            pltpu.VMEM((rows, cols), jnp.float32),
            dma((3,)),
            dma,
            dma,
            dma,
            dma,
            dma,
            dma((GROUPS,)),
            dma,
            dma,
        ],
        compiler_params=pltpu.CompilerParams(collective_id=0, has_side_effects=True),
    )(query, key, value, q_gain.reshape(1, HD), k_gain.reshape(1, HD), out_weight)


def solution(mesh):
    blks, ulys = mesh.shape["blk"], mesh.shape["uly"]
    tokens = P(("grp", "blk", "uly"), None)
    return jax.shard_map(
        functools.partial(on_device, blks, ulys),
        mesh=mesh,
        in_specs=(tokens, tokens, tokens, P(), P(), P("uly", None)),
        out_specs=tokens,
        check_vma=False,
    )
```

profile of v0, /device:TPU:0, one launch (start us, length us, event | category | flops | bytes accessed | tf_op | source)
XLA Modules:
  0.0 16.1 jit_solution(2110501981419019633)
XLA Ops:
  0.0 15.5 %shard_map.64 = bf16[16,2304]{1,0:T(8,128)(2,1)S(1)} custom-call(bf16[16,1152]{1,0:T(8,128)(2,1)} %q_hbm.1, bf16[16,1152]{1,0:T(8,128)(2,1)} %k_hbm.1, bf16[16,1152]{1,0:T(8,128)(2,1)} %v_hbm.1, f32[1,96]{1,0:T(1,128)} %bitcast.2, f32[1,96]{1,0:T(1,128)} %bitcast.3, bf16[576,2304]{1,0:T(8,128)(2,1)} %w_hbm.1), custom_call_target="tpu_custom_call" | custom-call | tf_op jit(solution)/shard_map/pallas_call | solution.py:244
  15.5 0.6 %copy.8 = bf16[16,2304]{1,0:T(8,128)(2,1)} copy(bf16[16,2304]{1,0:T(8,128)(2,1)S(1)} %shard_map.64) | data formatting | bytes 147456
where the time goes:
time: 16.3 us; the launch traced here: 16.1 us
  Pallas kernels  15.5 us (95%)
  local copies, waits for them, and re-layouts  0.64 us (4%)
    pallas_call x1, Pallas kernels, on_device(): pl.pallas_call(functools.partial(layer_kernel, blks, ulys, heads, copies)...  15.5 us
    unnamed x1, local copies, waits for them, and re-layouts  0.64 us

commit v1 on v0

--- a/solution.py
+++ b/solution.py
@@ -11,6 +11,7 @@
 LANES = 128
 CHUNKS = 1
 GROUPS = 4
+LOG2E = 1.4426950408889634
 MESH = pl.DeviceIdType.MESH
 
 
@@ -269,11 +270,356 @@
     )(query, key, value, q_gain.reshape(1, HD), k_gain.reshape(1, HD), out_weight)
 
 
+def pair_windows(width, heads):
+    tiles = width // LANES
+    span = (tiles + 1) // 2
+    half = heads // 2
+    sides = []
+    for side in range(2):
+        base = side * (tiles - span)
+        one = []
+        for j in range(half // 2):
+            lane = (side * half + 2 * j) * HD
+            tile = lane // LANES
+            one.append((tile - base, lane - tile * LANES))
+        sides.append(one)
+    return span * LANES, (tiles - span) * LANES, sides
+
+
+def gather_kernel(
+    blks, heads,
+    q_hbm, k_hbm, v_hbm, qg_hbm, kg_hbm, w_hbm, out_ref,
+    raw, gains, normed, kbuf, vbuf, qbuf, attn, back, acc, w_vmem,
+    load_sem, gain_sem, w_sem, send_v, send_k, send_q, send_a, send_w,
+    recv_v, recv_k, recv_q, recv_a, recv_w, ready, sib,
+):
+    levels = blks // 2
+    rows, width = raw.shape[1:]
+    span, shift, sides = pair_windows(width, heads)
+    group = 4 * rows
+    half_levels = levels // 2
+    part = half_levels * group
+    blk, uly = lax.axis_index("blk"), lax.axis_index("uly")
+    level, side = blk // 2, blk % 2
+    me = blk * 2 + uly
+    rank = level * 4 + side * 2 + 1 - uly
+    half = level // half_levels
+    owners = [(h, s, (half_levels - 1 + h) * 2 + s) for h in range(2) for s in range(2)]
+    owner_ranks = [2 * b for _, _, b in owners]
+    is_owner = functools.reduce(
+        jnp.logical_or, [jnp.logical_and(uly == 1, blk == b) for _, _, b in owners]
+    )
+    my_rows = pl.ds(pl.multiple_of(me * rows, rows), rows)
+    depth = w_hbm.shape[0]
+    my_depth = pl.ds(pl.multiple_of(uly * depth, depth), depth)
+
+    load_gains = [
+        pltpu.make_async_copy(src, gains.at[i], gain_sem)
+        for i, src in enumerate((qg_hbm, kg_hbm))
+    ]
+    loads = [
+        pltpu.make_async_copy(src, raw.at[i], load_sem.at[i])
+        for i, src in enumerate((q_hbm, k_hbm, v_hbm))
+    ]
+    for one in (loads[2], loads[1], *load_gains, loads[0]):
+        one.start()
+
+    barrier = pltpu.get_barrier_semaphore()
+    everyone = [(l, s, c) for l in range(levels) for s in range(2) for c in (1, 0)]
+    for l, s, c in everyone:
+        other = l * 4 + s * 2 + 1 - c
+        cond = other > rank
+        if other not in owner_ranks:
+            cond = jnp.logical_and(cond, jnp.logical_or(is_owner, blk == l * 2 + s))
+
+        @pl.when(cond)
+        def _(l=l, s=s, c=c):
+            pl.semaphore_signal(
+                barrier, inc=1, device_id={"blk": l * 2 + s, "uly": c}, device_id_type=MESH
+            )
+
+    load_w = pltpu.make_async_copy(w_hbm, w_vmem.at[my_depth], w_sem)
+    load_w.start()
+
+    heard = 1 - uly
+    for r in owner_ranks:
+        heard += jnp.logical_and(r < rank, r != rank - 1 + uly).astype(jnp.int32)
+    heard = jnp.where(is_owner, rank, heard)
+    pl.when(heard > 0)(lambda: pl.semaphore_wait(barrier, heard))
+
+    for l, s, c in everyone:
+        other = l * 4 + s * 2 + 1 - c
+
+        @pl.when(jnp.logical_and(other < rank, is_owner))
+        def _(l=l, s=s, c=c):
+            pl.semaphore_signal(
+                ready.at[blk], inc=1, device_id={"blk": l * 2 + s, "uly": c}, device_id_type=MESH
+            )
+
+    @pl.when(uly == 0)
+    def _():
+        pl.semaphore_signal(sib, inc=1, device_id={"uly": 1}, device_id_type=MESH)
+
+    def lanes(s):
+        return pl.ds(s * shift, span)
+
+    def give(src, dst, owner, send, recv):
+        _, s, b = owner
+        return pltpu.make_async_remote_copy(
+            src_ref=src.at[:, lanes(s)],
+            dst_ref=dst,
+            send_sem=send,
+            recv_sem=recv,
+            device_id={"blk": b, "uly": 1},
+            device_id_type=MESH,
+        )
+
+    def give_v(owner):
+        return give(raw.at[2], vbuf.at[my_rows], owner, send_v, recv_v.at[level])
+
+    def give_k(owner):
+        return give(normed.at[1], kbuf.at[my_rows], owner, send_k, recv_k.at[level])
+
+    q_rows = pl.ds(pl.multiple_of((me - half * (2 * blks // 2)) * rows, rows), rows)
+
+    def give_q(owner):
+        return give(normed.at[0], qbuf.at[q_rows], owner, send_q, recv_q)
+
+    def others(h, body):
+        for owner in owners[2 * h + 1], owners[2 * h]:
+            mine = jnp.logical_and(uly == 1, blk == owner[2])
+            pl.when(jnp.logical_not(mine))(functools.partial(body, owner))
+
+    def await_ready(h):
+        for _, _, b in owners[2 * h:2 * h + 2]:
+            pl.when(2 * b > rank)(lambda b=b: pl.semaphore_wait(ready.at[b], 1))
+
+    def normalize(i):
+        tiled = jnp.concatenate([gains[i]] * 4, axis=1)
+        lane = lax.broadcasted_iota(jnp.int32, (rows, LANES), 1)
+        for g in range(width // (3 * LANES)):
+            tiles = [
+                raw[i, :, (3 * g + t) * LANES:(3 * g + t + 1) * LANES].astype(jnp.float32)
+                for t in range(3)
+            ]
+            squares = [t * t for t in tiles]
+
+            def share(t, h):
+                low, high = h * HD - t * LANES, (h + 1) * HD - t * LANES
+                return jnp.logical_and(lane >= low, lane < high)
+
+            scales = []
+            for h in range(4):
+                parts = [
+                    jnp.where(share(t, h), squares[t], 0.0)
+                    for t in range(3)
+                    if h * HD < (t + 1) * LANES and (h + 1) * HD > t * LANES
+                ]
+                total = jnp.sum(functools.reduce(jnp.add, parts), axis=-1, keepdims=True)
+                scales.append(lax.rsqrt(total * (1.0 / HD) + 1e-06))
+            for t in range(3):
+                at = (3 * g + t) * LANES
+                scale = jnp.where(share(t, t), scales[t], scales[t + 1])
+                normed[i, :, at:at + LANES] = (
+                    tiles[t] * scale * tiled[:, t * LANES:(t + 1) * LANES]
+                ).astype(jnp.bfloat16)
+
+    loads[2].wait()
+    early = rank > owner_ranks[1]
+    pl.when(early)(lambda: others(0, lambda o: give_v(o).start()))
+    take(gains, gain_sem)
+    loads[1].wait()
+    normalize(1)
+    pl.when(early)(lambda: others(0, lambda o: give_k(o).start()))
+    loads[0].wait()
+    normalize(0)
+
+    @pl.when(jnp.logical_not(early))
+    def _():
+        await_ready(0)
+        others(0, lambda o: give_v(o).start())
+        others(0, lambda o: give_k(o).start())
+
+    pl.when(half == 0)(lambda: others(0, lambda o: give_q(o).start()))
+    give_w = pltpu.make_async_remote_copy(
+        src_ref=w_hbm,
+        dst_ref=w_vmem.at[my_depth],
+        send_sem=send_w,
+        recv_sem=recv_w,
+        device_id={"uly": 1 - uly},
+        device_id_type=MESH,
+    )
+
+    @pl.when(uly == 1)
+    def _():
+        pl.semaphore_wait(sib, 1)
+        give_w.start()
+
+    await_ready(1)
+    others(1, lambda o: give_v(o).start())
+    others(1, lambda o: give_k(o).start())
+    pl.when(half == 1)(lambda: others(1, lambda o: give_q(o).start()))
+    @pl.when(uly == 0)
+    def _():
+        give_w.start()
+
+    @pl.when(is_owner)
+    def _():
+        mine = pl.ds(pl.multiple_of(side * shift, LANES), span)
+        kbuf[my_rows, :] = normed[1, :, mine]
+        vbuf[my_rows, :] = raw[2, :, mine]
+        qbuf[q_rows, :] = normed[0, :, mine]
+        for l in range(levels):
+            @pl.when(l == level)
+            def _(l=l):
+                take(kbuf.at[pl.ds(0, 3 * rows)], recv_k.at[l])
+                take(vbuf.at[pl.ds(0, 3 * rows)], recv_v.at[l])
+
+            @pl.when(l != level)
+            def _(l=l):
+                take(kbuf.at[pl.ds(0, group)], recv_k.at[l])
+                take(vbuf.at[pl.ds(0, group)], recv_v.at[l])
+        take(qbuf.at[pl.ds(0, part - rows)], recv_q)
+
+        lane = lax.broadcasted_iota(jnp.int32, (part, 2 * LANES), 1)
+        attn[...] = jnp.zeros_like(attn)
+        for j in range(len(sides[0])):
+            (t0, o0), (t1, o1) = sides[0][j], sides[1][j]
+            off = o0 + side * (o1 - o0)
+            window = pl.ds(pl.multiple_of((t0 + side * (t1 - t0)) * LANES, LANES), 2 * LANES)
+            first = jnp.logical_and(lane >= off, lane < off + HD)
+            second = jnp.logical_and(lane >= off + HD, lane < off + 2 * HD)
+            query = qbuf[:, window]
+            zero = jnp.zeros_like(query)
+            query = jnp.concatenate(
+                [jnp.where(first, query, zero), jnp.where(second, query, zero)], axis=0
+            )
+            scores = lax.dot_general(
+                query, kbuf[:, window], (((1,), (1,)), ((), ())),
+                preferred_element_type=jnp.float32,
+            )
+            expd = jnp.exp2(scores * (float(HD) ** (-0.5) * LOG2E))
+            total = jnp.sum(expd, axis=-1, keepdims=True)
+            weighted = jnp.dot(
+                expd.astype(jnp.bfloat16), vbuf[:, window], preferred_element_type=jnp.float32
+            ) / total
+            both = jnp.where(first, weighted[:part], jnp.where(second, weighted[part:], 0.0))
+            attn[:, window] += both.astype(jnp.bfloat16)
+        for i in range(part // rows):
+            b, c = half * (blks // 2) + i // 2, i % 2
+            home = jnp.logical_and(b == blk, uly == c)
+
+            @pl.when(jnp.logical_not(home))
+            def _(i=i, b=b, c=c):
+                pltpu.make_async_remote_copy(
+                    src_ref=attn.at[pl.ds(i * rows, rows)],
+                    dst_ref=back.at[side],
+                    send_sem=send_a,
+                    recv_sem=recv_a.at[side],
+                    device_id={"blk": b, "uly": c},
+                    device_id_type=MESH,
+                ).start()
+
+        back[side] = attn[q_rows, :]
+
+    load_w.wait()
+    give_w.wait_recv()
+
+    @pl.when(jnp.logical_not(is_owner))
+    def _():
+        take(back.at[0], recv_a.at[side])
+
+    def project(s):
+        return jnp.dot(
+            back[s],
+            w_vmem[pl.ds(pl.multiple_of(s * shift, LANES), span), :],
+            preferred_element_type=jnp.float32,
+        )
+
+    acc[...] = project(side)
+    take(back.at[0], recv_a.at[1 - side])
+    out_ref[...] = (acc[...] + project(1 - side)).astype(out_ref.dtype)
+
+    give_w.wait_send()
+    slab = qbuf.at[pl.ds(0, rows)]
+    for i in range(3):
+        take(slab, send_v)
+        take(slab, send_k)
+    take(slab, send_q)
+
+    @pl.when(is_owner)
+    def _():
+        for i in range(part // rows - 1):
+            take(slab, send_a)
+
+    @pl.when(jnp.logical_not(is_owner))
+    def _():
+        for sem in (send_v, send_k, send_q):
+            take(slab, sem)
+
+
+def on_device_gather(blks, query, key, value, q_gain, k_gain, out_weight):
+    rows, width = query.shape
+    heads = width // HD
+    depth, cols = out_weight.shape
+    levels = blks // 2
+    seq = 2 * blks * rows
+    span = pair_windows(width, heads)[0]
+    dma = pltpu.SemaphoreType.DMA
+    bf16 = jnp.bfloat16
+    return pl.pallas_call(
+        functools.partial(gather_kernel, blks, heads),
+        out_shape=pltpu.VMEM((rows, cols), bf16),
+        in_specs=[pl.BlockSpec(memory_space=pltpu.HBM)] * 6,
+        out_specs=pl.BlockSpec(memory_space=pltpu.VMEM),
+        scratch_shapes=[
+            pltpu.VMEM((3, rows, width), bf16),
+            pltpu.VMEM((2, 1, HD), jnp.float32),
+            pltpu.VMEM((2, rows, width), bf16),
+            pltpu.VMEM((seq, span), bf16),
+            pltpu.VMEM((seq, span), bf16),
+            pltpu.VMEM((seq // 2, span), bf16),
+            pltpu.VMEM((seq // 2, span), bf16),
+            pltpu.VMEM((2, rows, span), bf16),
+            pltpu.VMEM((rows, cols), jnp.float32),
+            pltpu.VMEM((width, cols), bf16),
+            dma((3,)),
+            dma, dma, dma, dma, dma, dma, dma,
+            dma((levels,)),
+            dma((levels,)),
+            dma,
+            dma((2,)),
+            dma,
+            pltpu.SemaphoreType.REGULAR((blks,)),
+            pltpu.SemaphoreType.REGULAR,
+        ],
+        compiler_params=pltpu.CompilerParams(collective_id=0, has_side_effects=True),
+    )(query, key, value, q_gain.reshape(1, HD), k_gain.reshape(1, HD), out_weight)
+
+
+def fits_gather(blks, ulys, width):
+    heads = width // HD
+    return (
+        ulys == 2
+        and blks % 4 == 0
+        and heads % 4 == 0
+        and width % (3 * LANES) == 0
+        and (width // LANES) % 2 == 1
+        and blks <= heads
+    )
+
+
 def solution(mesh):
     blks, ulys = mesh.shape["blk"], mesh.shape["uly"]
     tokens = P(("grp", "blk", "uly"), None)
+
+    def body(query, *rest):
+        if fits_gather(blks, ulys, query.shape[1]):
+            return on_device_gather(blks, query, *rest)
+        return on_device(blks, ulys, query, *rest)
+
     return jax.shard_map(
-        functools.partial(on_device, blks, ulys),
+        body,
         mesh=mesh,
         in_specs=(tokens, tokens, tokens, P(), P(), P("uly", None)),
         out_specs=tokens,

time: 16.3 us -> 14.8 us (0.908)
  Pallas kernels: 15.5 us -> 14 us
    pallas_call x1, Pallas kernels: 15.5 us -> 14 us  [on_device_gather(): pl.pallas_call(functools.partial(gather_kernel, blks, heads), out_shape=p...]
where the time goes in v1:
time: 14.8 us; the launch traced here: 14.7 us
  Pallas kernels  14 us (95%)
  local copies, waits for them, and re-layouts  0.64 us (4%)
    pallas_call x1, Pallas kernels, on_device_gather(): pl.pallas_call(functools.partial(gather_kernel, blks, heads), out_shape=p...  14 us
    unnamed x1, local copies, waits for them, and re-layouts  0.64 us

profile of v1, /device:TPU:0, one launch (start us, length us, event | category | flops | bytes accessed | tf_op | source)
XLA Modules:
  0.0 14.7 jit_solution(14041743144251146504)
XLA Ops:
  0.0 14.0 %shard_map.64 = bf16[16,2304]{1,0:T(8,128)(2,1)S(1)} custom-call(bf16[16,1152]{1,0:T(8,128)(2,1)} %q_hbm.1, bf16[16,1152]{1,0:T(8,128)(2,1)} %k_hbm.1, bf16[16,1152]{1,0:T(8,128)(2,1)} %v_hbm.1, f32[1,96]{1,0:T(1,128)} %bitcast.2, f32[1,96]{1,0:T(1,128)} %bitcast.3, bf16[576,2304]{1,0:T(8,128)(2,1)} %w_hbm.1), custom_call_target="tpu_custom_call" | custom-call | tf_op jit(solution)/shard_map/pallas_call | solution.py:570
  14.0 0.6 %copy.8 = bf16[16,2304]{1,0:T(8,128)(2,1)} copy(bf16[16,2304]{1,0:T(8,128)(2,1)S(1)} %shard_map.64) | data formatting | bytes 147456

commit v2 on v1

--- a/solution.py
+++ b/solution.py
@@ -291,7 +291,7 @@
     q_hbm, k_hbm, v_hbm, qg_hbm, kg_hbm, w_hbm, out_ref,
     raw, gains, normed, kbuf, vbuf, qbuf, attn, back, acc, w_vmem,
     load_sem, gain_sem, w_sem, send_v, send_k, send_q, send_a, send_w,
-    recv_v, recv_k, recv_q, recv_a, recv_w, ready, sib,
+    recv_v, recv_k, recv_q, recv_a, recv_w, ready,
 ):
     levels = blks // 2
     rows, width = raw.shape[1:]
@@ -302,10 +302,8 @@
     blk, uly = lax.axis_index("blk"), lax.axis_index("uly")
     level, side = blk // 2, blk % 2
     me = blk * 2 + uly
-    rank = level * 4 + side * 2 + 1 - uly
     half = level // half_levels
     owners = [(h, s, (half_levels - 1 + h) * 2 + s) for h in range(2) for s in range(2)]
-    owner_ranks = [2 * b for _, _, b in owners]
     is_owner = functools.reduce(
         jnp.logical_or, [jnp.logical_and(uly == 1, blk == b) for _, _, b in owners]
     )
@@ -325,52 +323,45 @@
         one.start()
 
     barrier = pltpu.get_barrier_semaphore()
-    everyone = [(l, s, c) for l in range(levels) for s in range(2) for c in (1, 0)]
-    for l, s, c in everyone:
-        other = l * 4 + s * 2 + 1 - c
-        cond = other > rank
-        if other not in owner_ranks:
-            cond = jnp.logical_and(cond, jnp.logical_or(is_owner, blk == l * 2 + s))
+    late = half == 1
+    for d in range(2 * blks):
+        b, c = d // 2, d % 2
+        cond = jnp.logical_or(
+            jnp.logical_and(blk == b, uly == 1 - c),
+            jnp.logical_and(is_owner, me != d if b >= blks // 2 else jnp.logical_and(me != d, jnp.logical_not(late))),
+        )
+        if c == 1 and b in [o[2] for o in owners[2:]]:
+            cond = jnp.logical_or(cond, jnp.logical_not(late))
 
         @pl.when(cond)
-        def _(l=l, s=s, c=c):
+        def _(b=b, c=c):
             pl.semaphore_signal(
-                barrier, inc=1, device_id={"blk": l * 2 + s, "uly": c}, device_id_type=MESH
+                barrier, inc=1, device_id={"blk": b, "uly": c}, device_id_type=MESH
             )
 
     load_w = pltpu.make_async_copy(w_hbm, w_vmem.at[my_depth], w_sem)
     load_w.start()
 
-    heard = 1 - uly
-    for r in owner_ranks:
-        heard += jnp.logical_and(r < rank, r != rank - 1 + uly).astype(jnp.int32)
-    heard = jnp.where(is_owner, rank, heard)
-    pl.when(heard > 0)(lambda: pl.semaphore_wait(barrier, heard))
-
-    for l, s, c in everyone:
-        other = l * 4 + s * 2 + 1 - c
-
-        @pl.when(jnp.logical_and(other < rank, is_owner))
-        def _(l=l, s=s, c=c):
+    owner_here = functools.reduce(jnp.logical_or, [blk == b for _, _, b in owners])
+    heard = 3 + 2 * half - owner_here.astype(jnp.int32)
+    heard += jnp.where(jnp.logical_and(is_owner, late), blks - 2, 0)
+    pl.semaphore_wait(barrier, heard)
+
+    @pl.when(jnp.logical_and(is_owner, late))
+    def _():
+        for d in range(blks):
             pl.semaphore_signal(
-                ready.at[blk], inc=1, device_id={"blk": l * 2 + s, "uly": c}, device_id_type=MESH
+                ready.at[side], inc=1, device_id={"blk": d // 2, "uly": d % 2}, device_id_type=MESH
             )
 
-    @pl.when(uly == 0)
-    def _():
-        pl.semaphore_signal(sib, inc=1, device_id={"uly": 1}, device_id_type=MESH)
-
-    def lanes(s):
-        return pl.ds(s * shift, span)
-
     def give(src, dst, owner, send, recv):
-        _, s, b = owner
+        h, s = owner
         return pltpu.make_async_remote_copy(
-            src_ref=src.at[:, lanes(s)],
+            src_ref=src.at[:, pl.ds(pl.multiple_of(s * shift, LANES), span)],
             dst_ref=dst,
             send_sem=send,
             recv_sem=recv,
-            device_id={"blk": b, "uly": 1},
+            device_id={"blk": (half_levels - 1 + h) * 2 + s, "uly": 1},
             device_id_type=MESH,
         )
 
@@ -386,13 +377,9 @@
         return give(normed.at[0], qbuf.at[q_rows], owner, send_q, recv_q)
 
     def others(h, body):
-        for owner in owners[2 * h + 1], owners[2 * h]:
-            mine = jnp.logical_and(uly == 1, blk == owner[2])
-            pl.when(jnp.logical_not(mine))(functools.partial(body, owner))
-
-    def await_ready(h):
-        for _, _, b in owners[2 * h:2 * h + 2]:
-            pl.when(2 * b > rank)(lambda b=b: pl.semaphore_wait(ready.at[b], 1))
+        body((h, 1 - side))
+        mine = jnp.logical_and(uly == 1, blk == (half_levels - 1 + h) * 2 + side)
+        pl.when(jnp.logical_not(mine))(lambda: body((h, side)))
 
     def normalize(i):
         tiled = jnp.concatenate([gains[i]] * 4, axis=1)
@@ -425,22 +412,23 @@
                 ).astype(jnp.bfloat16)
 
     loads[2].wait()
-    early = rank > owner_ranks[1]
-    pl.when(early)(lambda: others(0, lambda o: give_v(o).start()))
+    others(0, lambda o: give_v(o).start())
     take(gains, gain_sem)
     loads[1].wait()
     normalize(1)
-    pl.when(early)(lambda: others(0, lambda o: give_k(o).start()))
+    others(0, lambda o: give_k(o).start())
     loads[0].wait()
     normalize(0)
-
-    @pl.when(jnp.logical_not(early))
-    def _():
-        await_ready(0)
-        others(0, lambda o: give_v(o).start())
-        others(0, lambda o: give_k(o).start())
-
     pl.when(half == 0)(lambda: others(0, lambda o: give_q(o).start()))
+
+    @pl.when(jnp.logical_not(late))
+    def _():
+        for i in range(2):
+            pl.semaphore_wait(ready.at[i], 1)
+
+    others(1, lambda o: give_v(o).start())
+    others(1, lambda o: give_k(o).start())
+    pl.when(half == 1)(lambda: others(1, lambda o: give_q(o).start()))
     give_w = pltpu.make_async_remote_copy(
         src_ref=w_hbm,
         dst_ref=w_vmem.at[my_depth],
@@ -450,18 +438,7 @@
         device_id_type=MESH,
     )
 
-    @pl.when(uly == 1)
-    def _():
-        pl.semaphore_wait(sib, 1)
-        give_w.start()
-
-    await_ready(1)
-    others(1, lambda o: give_v(o).start())
-    others(1, lambda o: give_k(o).start())
-    pl.when(half == 1)(lambda: others(1, lambda o: give_q(o).start()))
-    @pl.when(uly == 0)
-    def _():
-        give_w.start()
+    give_w.start()
 
     @pl.when(is_owner)
     def _():
@@ -590,8 +567,7 @@
             dma,
             dma((2,)),
             dma,
-            pltpu.SemaphoreType.REGULAR((blks,)),
-            pltpu.SemaphoreType.REGULAR,
+            pltpu.SemaphoreType.REGULAR((2,)),
         ],
         compiler_params=pltpu.CompilerParams(collective_id=0, has_side_effects=True),
     )(query, key, value, q_gain.reshape(1, HD), k_gain.reshape(1, HD), out_weight)

time: 14.8 us -> 14.2 us (0.959)
  Pallas kernels: 14 us -> 13.4 us
    pallas_call x1, Pallas kernels: 14 us -> 13.4 us  [on_device_gather(): pl.pallas_call(functools.partial(gather_kernel, blks, heads), out_shape=p...]
where the time goes in v2:
time: 14.2 us; the launch traced here: 14 us
  Pallas kernels  13.4 us (94%)
  local copies, waits for them, and re-layouts  0.64 us (5%)
    pallas_call x1, Pallas kernels, on_device_gather(): pl.pallas_call(functools.partial(gather_kernel, blks, heads), out_shape=p...  13.4 us
    unnamed x1, local copies, waits for them, and re-layouts  0.64 us

profile of v2, /device:TPU:0, one launch (start us, length us, event | category | flops | bytes accessed | tf_op | source)
XLA Modules:
  0.0 14.0 jit_solution(13396524963960948319)
XLA Ops:
  0.0 13.4 %shard_map.64 = bf16[16,2304]{1,0:T(8,128)(2,1)S(1)} custom-call(bf16[16,1152]{1,0:T(8,128)(2,1)} %q_hbm.1, bf16[16,1152]{1,0:T(8,128)(2,1)} %k_hbm.1, bf16[16,1152]{1,0:T(8,128)(2,1)} %v_hbm.1, f32[1,96]{1,0:T(1,128)} %bitcast.2, f32[1,96]{1,0:T(1,128)} %bitcast.3, bf16[576,2304]{1,0:T(8,128)(2,1)} %w_hbm.1), custom_call_target="tpu_custom_call" | custom-call | tf_op jit(solution)/shard_map/pallas_call | solution.py:547
  13.4 0.6 %copy.8 = bf16[16,2304]{1,0:T(8,128)(2,1)} copy(bf16[16,2304]{1,0:T(8,128)(2,1)S(1)} %shard_map.64) | data formatting | bytes 147456

commit v3 on v2

--- a/solution.py
+++ b/solution.py
@@ -270,32 +270,17 @@
     )(query, key, value, q_gain.reshape(1, HD), k_gain.reshape(1, HD), out_weight)
 
 
-def pair_windows(width, heads):
-    tiles = width // LANES
-    span = (tiles + 1) // 2
-    half = heads // 2
-    sides = []
-    for side in range(2):
-        base = side * (tiles - span)
-        one = []
-        for j in range(half // 2):
-            lane = (side * half + 2 * j) * HD
-            tile = lane // LANES
-            one.append((tile - base, lane - tile * LANES))
-        sides.append(one)
-    return span * LANES, (tiles - span) * LANES, sides
-
-
 def gather_kernel(
     blks, heads,
     q_hbm, k_hbm, v_hbm, qg_hbm, kg_hbm, w_hbm, out_ref,
-    raw, gains, normed, kbuf, vbuf, qbuf, attn, back, acc, w_vmem,
-    load_sem, gain_sem, w_sem, send_v, send_k, send_q, send_a, send_w,
-    recv_v, recv_k, recv_q, recv_a, recv_w, ready,
+    raw, gains, k_four, kv_two, q_all, kbuf, vbuf, tbuf, qbuf, four, two, back4, back2, acc, w_vmem,
+    load_sem, gain_sem, w_sem, send_kv, send_q, send4, send2, send_w,
+    recv_kv, recv_q, recv4, recv2, recv_w, ready,
 ):
     levels = blks // 2
     rows, width = raw.shape[1:]
-    span, shift, sides = pair_windows(width, heads)
+    wide, pair = 4 * HD, 2 * HD
+    last = width - wide
     group = 4 * rows
     half_levels = levels // 2
     part = half_levels * group
@@ -357,7 +342,7 @@
     def give(src, dst, owner, send, recv):
         h, s = owner
         return pltpu.make_async_remote_copy(
-            src_ref=src.at[:, pl.ds(pl.multiple_of(s * shift, LANES), span)],
+            src_ref=src,
             dst_ref=dst,
             send_sem=send,
             recv_sem=recv,
@@ -365,60 +350,80 @@
             device_id_type=MESH,
         )
 
+    def v_four(s):
+        return raw.at[2, :, pl.ds(pl.multiple_of(s * last, LANES), wide)]
+
     def give_v(owner):
-        return give(raw.at[2], vbuf.at[my_rows], owner, send_v, recv_v.at[level])
+        return give(v_four(owner[1]), vbuf.at[my_rows], owner, send_kv, recv_kv.at[0, level])
 
     def give_k(owner):
-        return give(normed.at[1], kbuf.at[my_rows], owner, send_k, recv_k.at[level])
+        return give(k_four.at[owner[1]], kbuf.at[my_rows], owner, send_kv, recv_kv.at[1, level])
+
+    def give_two(owner):
+        return give(kv_two.at[owner[1]], tbuf.at[my_rows], owner, send_kv, recv_kv.at[2, level])
 
     q_rows = pl.ds(pl.multiple_of((me - half * (2 * blks // 2)) * rows, rows), rows)
 
     def give_q(owner):
-        return give(normed.at[0], qbuf.at[q_rows], owner, send_q, recv_q)
+        return give(q_all.at[owner[1]], qbuf.at[q_rows], owner, send_q, recv_q)
 
     def others(h, body):
         body((h, 1 - side))
         mine = jnp.logical_and(uly == 1, blk == (half_levels - 1 + h) * 2 + side)
         pl.when(jnp.logical_not(mine))(lambda: body((h, side)))
 
-    def normalize(i):
+    def normalize(i, g):
         tiled = jnp.concatenate([gains[i]] * 4, axis=1)
         lane = lax.broadcasted_iota(jnp.int32, (rows, LANES), 1)
-        for g in range(width // (3 * LANES)):
-            tiles = [
-                raw[i, :, (3 * g + t) * LANES:(3 * g + t + 1) * LANES].astype(jnp.float32)
+        tiles = [
+            raw[i, :, (3 * g + t) * LANES:(3 * g + t + 1) * LANES].astype(jnp.float32)
+            for t in range(3)
+        ]
+        squares = [t * t for t in tiles]
+
+        def share(t, h):
+            low, high = h * HD - t * LANES, (h + 1) * HD - t * LANES
+            return jnp.logical_and(lane >= low, lane < high)
+
+        scales = []
+        for h in range(4):
+            parts = [
+                jnp.where(share(t, h), squares[t], 0.0)
                 for t in range(3)
+                if h * HD < (t + 1) * LANES and (h + 1) * HD > t * LANES
             ]
-            squares = [t * t for t in tiles]
-
-            def share(t, h):
-                low, high = h * HD - t * LANES, (h + 1) * HD - t * LANES
-                return jnp.logical_and(lane >= low, lane < high)
-
-            scales = []
-            for h in range(4):
-                parts = [
-                    jnp.where(share(t, h), squares[t], 0.0)
-                    for t in range(3)
-                    if h * HD < (t + 1) * LANES and (h + 1) * HD > t * LANES
-                ]
-                total = jnp.sum(functools.reduce(jnp.add, parts), axis=-1, keepdims=True)
-                scales.append(lax.rsqrt(total * (1.0 / HD) + 1e-06))
-            for t in range(3):
-                at = (3 * g + t) * LANES
-                scale = jnp.where(share(t, t), scales[t], scales[t + 1])
-                normed[i, :, at:at + LANES] = (
-                    tiles[t] * scale * tiled[:, t * LANES:(t + 1) * LANES]
-                ).astype(jnp.bfloat16)
+            total = jnp.sum(functools.reduce(jnp.add, parts), axis=-1, keepdims=True)
+            scales.append(lax.rsqrt(total * (1.0 / HD) + 1e-06))
+        return jnp.concatenate(
+            [
+                tiles[t]
+                * jnp.where(share(t, t), scales[t], scales[t + 1])
+                * tiled[:, t * LANES:(t + 1) * LANES]
+                for t in range(3)
+            ],
+            axis=1,
+        ).astype(jnp.bfloat16)
 
     loads[2].wait()
     others(0, lambda o: give_v(o).start())
     take(gains, gain_sem)
     loads[1].wait()
-    normalize(1)
+    for s in range(2):
+        k_four[s] = normalize(1, 2 * s)
     others(0, lambda o: give_k(o).start())
+    middle = normalize(1, 1)
+    for s in range(2):
+        kv_two[s] = jnp.concatenate(
+            [middle[:, s * pair:(s + 1) * pair], raw[2, :, wide + s * pair:wide + (s + 1) * pair]],
+            axis=1,
+        )
+    others(0, lambda o: give_two(o).start())
     loads[0].wait()
-    normalize(0)
+    middle = normalize(0, 1)
+    pad = jnp.zeros((rows, 2 * LANES - pair), jnp.bfloat16)
+    for s in range(2):
+        q_all[s, :, 0:wide] = normalize(0, 2 * s)
+        q_all[s, :, wide:] = jnp.concatenate([middle[:, s * pair:(s + 1) * pair], pad], axis=1)
     pl.when(half == 0)(lambda: others(0, lambda o: give_q(o).start()))
 
     @pl.when(jnp.logical_not(late))
@@ -426,8 +431,8 @@
         for i in range(2):
             pl.semaphore_wait(ready.at[i], 1)
 
-    others(1, lambda o: give_v(o).start())
-    others(1, lambda o: give_k(o).start())
+    for one in (give_v, give_k, give_two):
+        others(1, lambda o, one=one: one(o).start())
     pl.when(half == 1)(lambda: others(1, lambda o: give_q(o).start()))
     give_w = pltpu.make_async_remote_copy(
         src_ref=w_hbm,
@@ -442,97 +447,122 @@
 
     @pl.when(is_owner)
     def _():
-        mine = pl.ds(pl.multiple_of(side * shift, LANES), span)
-        kbuf[my_rows, :] = normed[1, :, mine]
-        vbuf[my_rows, :] = raw[2, :, mine]
-        qbuf[q_rows, :] = normed[0, :, mine]
-        for l in range(levels):
-            @pl.when(l == level)
-            def _(l=l):
-                take(kbuf.at[pl.ds(0, 3 * rows)], recv_k.at[l])
-                take(vbuf.at[pl.ds(0, 3 * rows)], recv_v.at[l])
-
-            @pl.when(l != level)
-            def _(l=l):
-                take(kbuf.at[pl.ds(0, group)], recv_k.at[l])
-                take(vbuf.at[pl.ds(0, group)], recv_v.at[l])
-        take(qbuf.at[pl.ds(0, part - rows)], recv_q)
+        kbuf[my_rows, :] = k_four[side]
+        vbuf[my_rows, :] = v_four(side)[...]
+        tbuf[my_rows, :] = kv_two[side]
+        qbuf[q_rows, :] = q_all[side]
+
+        def gathered(i, buf):
+            for l in range(levels):
+                @pl.when(l == level)
+                def _(l=l):
+                    take(buf.at[pl.ds(0, 3 * rows)], recv_kv.at[i, l])
+
+                @pl.when(l != level)
+                def _(l=l):
+                    take(buf.at[pl.ds(0, group)], recv_kv.at[i, l])
 
         lane = lax.broadcasted_iota(jnp.int32, (part, 2 * LANES), 1)
-        attn[...] = jnp.zeros_like(attn)
-        for j in range(len(sides[0])):
-            (t0, o0), (t1, o1) = sides[0][j], sides[1][j]
-            off = o0 + side * (o1 - o0)
-            window = pl.ds(pl.multiple_of((t0 + side * (t1 - t0)) * LANES, LANES), 2 * LANES)
-            first = jnp.logical_and(lane >= off, lane < off + HD)
-            second = jnp.logical_and(lane >= off + HD, lane < off + 2 * HD)
-            query = qbuf[:, window]
+
+        def heads_at(off):
+            return (
+                jnp.logical_and(lane >= off, lane < off + HD),
+                jnp.logical_and(lane >= off + HD, lane < off + 2 * HD),
+            )
+
+        def attend(query, off, keys, values, value_off):
+            first, second = heads_at(off)
             zero = jnp.zeros_like(query)
             query = jnp.concatenate(
                 [jnp.where(first, query, zero), jnp.where(second, query, zero)], axis=0
             )
             scores = lax.dot_general(
-                query, kbuf[:, window], (((1,), (1,)), ((), ())),
-                preferred_element_type=jnp.float32,
+                query, keys, (((1,), (1,)), ((), ())), preferred_element_type=jnp.float32
             )
             expd = jnp.exp2(scores * (float(HD) ** (-0.5) * LOG2E))
             total = jnp.sum(expd, axis=-1, keepdims=True)
             weighted = jnp.dot(
-                expd.astype(jnp.bfloat16), vbuf[:, window], preferred_element_type=jnp.float32
-            ) / total
-            both = jnp.where(first, weighted[:part], jnp.where(second, weighted[part:], 0.0))
-            attn[:, window] += both.astype(jnp.bfloat16)
-        for i in range(part // rows):
-            b, c = half * (blks // 2) + i // 2, i % 2
-            home = jnp.logical_and(b == blk, uly == c)
-
-            @pl.when(jnp.logical_not(home))
-            def _(i=i, b=b, c=c):
-                pltpu.make_async_remote_copy(
-                    src_ref=attn.at[pl.ds(i * rows, rows)],
-                    dst_ref=back.at[side],
-                    send_sem=send_a,
-                    recv_sem=recv_a.at[side],
-                    device_id={"blk": b, "uly": c},
-                    device_id_type=MESH,
-                ).start()
-
-        back[side] = attn[q_rows, :]
+                expd.astype(jnp.bfloat16), values, preferred_element_type=jnp.float32
+            ) * (1.0 / total)
+            first, second = heads_at(value_off)
+            return jnp.where(first, weighted[:part], jnp.where(second, weighted[part:], 0.0))
+
+        def send_back(src, dst, send, recv):
+            for i in range(part // rows):
+                b, c = half * (blks // 2) + i // 2, i % 2
+                home = jnp.logical_and(b == blk, uly == c)
+
+                @pl.when(jnp.logical_not(home))
+                def _(i=i, b=b, c=c):
+                    pltpu.make_async_remote_copy(
+                        src_ref=src.at[pl.ds(i * rows, rows)],
+                        dst_ref=dst.at[side],
+                        send_sem=send,
+                        recv_sem=recv.at[side],
+                        device_id={"blk": b, "uly": c},
+                        device_id_type=MESH,
+                    ).start()
+
+            dst[side] = src[q_rows, :]
+
+        take(qbuf.at[pl.ds(0, part - rows)], recv_q)
+        gathered(0, vbuf)
+        gathered(1, kbuf)
+        low = attend(qbuf[:, 0:2 * LANES], 0, kbuf[:, 0:2 * LANES], vbuf[:, 0:2 * LANES], 0)
+        high = attend(
+            qbuf[:, LANES:wide], pair - LANES, kbuf[:, LANES:wide], vbuf[:, LANES:wide], pair - LANES
+        )
+        four[...] = jnp.concatenate(
+            [low[:, :LANES], low[:, LANES:] + high[:, :LANES], high[:, LANES:]], axis=1
+        ).astype(jnp.bfloat16)
+        send_back(four, back4, send4, recv4)
+        gathered(2, tbuf)
+        two[...] = attend(
+            qbuf[:, wide:], 0, tbuf[:, 0:2 * LANES], tbuf[:, LANES:], pair - LANES
+        ).astype(jnp.bfloat16)
+        send_back(two, back2, send2, recv2)
 
     load_w.wait()
     give_w.wait_recv()
 
-    @pl.when(jnp.logical_not(is_owner))
-    def _():
-        take(back.at[0], recv_a.at[side])
-
-    def project(s):
+    def project(back, recv, s, start, own):
+        if own:
+            pl.when(jnp.logical_not(is_owner))(lambda: take(back.at[0], recv.at[s]))
+        else:
+            take(back.at[0], recv.at[s])
         return jnp.dot(
             back[s],
-            w_vmem[pl.ds(pl.multiple_of(s * shift, LANES), span), :],
+            w_vmem[pl.ds(pl.multiple_of(start, LANES // 2), back.shape[2]), :],
             preferred_element_type=jnp.float32,
         )
 
-    acc[...] = project(side)
-    take(back.at[0], recv_a.at[1 - side])
-    out_ref[...] = (acc[...] + project(1 - side)).astype(out_ref.dtype)
+    def project4(s, own):
+        return project(back4, recv4, s, s * last, own)
+
+    def project2(s, own):
+        return project(back2, recv2, s, wide + LANES - pair + s * pair, own)
+
+    acc[...] = project4(side, True)
+    acc[...] += project4(1 - side, False)
+    acc[...] += project2(side, True)
+    out_ref[...] = (acc[...] + project2(1 - side, False)).astype(out_ref.dtype)
 
     give_w.wait_send()
-    slab = qbuf.at[pl.ds(0, rows)]
-    for i in range(3):
-        take(slab, send_v)
-        take(slab, send_k)
-    take(slab, send_q)
+    slab = tbuf.at[pl.ds(0, rows)]
+    for i in range(9):
+        take(slab, send_kv)
+    take(qbuf.at[pl.ds(0, rows)], send_q)
 
     @pl.when(is_owner)
     def _():
-        for i in range(part // rows - 1):
-            take(slab, send_a)
+        take(four.at[pl.ds(0, part - rows)], send4)
+        take(two.at[pl.ds(0, part - rows)], send2)
 
     @pl.when(jnp.logical_not(is_owner))
     def _():
-        for sem in (send_v, send_k, send_q):
-            take(slab, sem)
+        for i in range(3):
+            take(slab, send_kv)
+        take(qbuf.at[pl.ds(0, rows)], send_q)
 
 
 def on_device_gather(blks, query, key, value, q_gain, k_gain, out_weight):
@@ -541,7 +571,7 @@
     depth, cols = out_weight.shape
     levels = blks // 2
     seq = 2 * blks * rows
-    span = pair_windows(width, heads)[0]
+    wide, pair, two = 4 * HD, 2 * HD, 2 * LANES
     dma = pltpu.SemaphoreType.DMA
     bf16 = jnp.bfloat16
     return pl.pallas_call(
@@ -552,19 +582,24 @@
         scratch_shapes=[
             pltpu.VMEM((3, rows, width), bf16),
             pltpu.VMEM((2, 1, HD), jnp.float32),
-            pltpu.VMEM((2, rows, width), bf16),
-            pltpu.VMEM((seq, span), bf16),
-            pltpu.VMEM((seq, span), bf16),
-            pltpu.VMEM((seq // 2, span), bf16),
-            pltpu.VMEM((seq // 2, span), bf16),
-            pltpu.VMEM((2, rows, span), bf16),
+            pltpu.VMEM((2, rows, wide), bf16),
+            pltpu.VMEM((2, rows, 2 * pair), bf16),
+            pltpu.VMEM((2, rows, wide + two), bf16),
+            pltpu.VMEM((seq, wide), bf16),
+            pltpu.VMEM((seq, wide), bf16),
+            pltpu.VMEM((seq, 2 * pair), bf16),
+            pltpu.VMEM((seq // 2, wide + two), bf16),
+            pltpu.VMEM((seq // 2, wide), bf16),
+            pltpu.VMEM((seq // 2, two), bf16),
+            pltpu.VMEM((2, rows, wide), bf16),
+            pltpu.VMEM((2, rows, two), bf16),
             pltpu.VMEM((rows, cols), jnp.float32),
             pltpu.VMEM((width, cols), bf16),
             dma((3,)),
             dma, dma, dma, dma, dma, dma, dma,
-            dma((levels,)),
-            dma((levels,)),
-            dma,
+            dma((3, levels)),
+            dma,
+            dma((2,)),
             dma((2,)),
             dma,
             pltpu.SemaphoreType.REGULAR((2,)),
@@ -575,14 +610,7 @@
 
 def fits_gather(blks, ulys, width):
     heads = width // HD
-    return (
-        ulys == 2
-        and blks % 4 == 0
-        and heads % 4 == 0
-        and width % (3 * LANES) == 0
-        and (width // LANES) % 2 == 1
-        and blks <= heads
-    )
+    return ulys == 2 and blks % 4 == 0 and blks <= heads and heads // 2 == 6 and width % LANES == 0
 
 
 def solution(mesh):

time: 14.2 us -> 13.4 us (0.944)
  Pallas kernels: 13.4 us -> 12.6 us
    pallas_call x1, Pallas kernels: 13.4 us -> 12.6 us  [on_device_gather(): pl.pallas_call(functools.partial(gather_kernel, blks, heads), out_shape=p...]
where the time goes in v3:
time: 13.4 us; the launch traced here: 13.3 us
  Pallas kernels  12.6 us (94%)
  local copies, waits for them, and re-layouts  0.64 us (5%)
    pallas_call x1, Pallas kernels, on_device_gather(): pl.pallas_call(functools.partial(gather_kernel, blks, heads), out_shape=p...  12.6 us
    unnamed x1, local copies, waits for them, and re-layouts  0.64 us

profile of v3, /device:TPU:0, one launch (start us, length us, event | category | flops | bytes accessed | tf_op | source)
XLA Modules:
  0.0 13.3 jit_solution(1932900332675647849)
XLA Ops:
  0.0 12.6 %shard_map.64 = bf16[16,2304]{1,0:T(8,128)(2,1)S(1)} custom-call(bf16[16,1152]{1,0:T(8,128)(2,1)} %q_hbm.1, bf16[16,1152]{1,0:T(8,128)(2,1)} %k_hbm.1, bf16[16,1152]{1,0:T(8,128)(2,1)} %v_hbm.1, f32[1,96]{1,0:T(1,128)} %bitcast.2, f32[1,96]{1,0:T(1,128)} %bitcast.3, bf16[576,2304]{1,0:T(8,128)(2,1)} %w_hbm.1), custom_call_target="tpu_custom_call" | custom-call | tf_op jit(solution)/shard_map/pallas_call | solution.py:577
  12.7 0.6 %copy.8 = bf16[16,2304]{1,0:T(8,128)(2,1)} copy(bf16[16,2304]{1,0:T(8,128)(2,1)S(1)} %shard_map.64) | data formatting | bytes 147456

commit v4 on v3

--- a/solution.py
+++ b/solution.py
@@ -354,23 +354,31 @@
         return raw.at[2, :, pl.ds(pl.multiple_of(s * last, LANES), wide)]
 
     def give_v(owner):
-        return give(v_four(owner[1]), vbuf.at[my_rows], owner, send_kv, recv_kv.at[0, level])
+        return give(v_four(owner[1]), vbuf.at[my_rows], owner, send_kv, recv_kv.at[0])
 
     def give_k(owner):
-        return give(k_four.at[owner[1]], kbuf.at[my_rows], owner, send_kv, recv_kv.at[1, level])
+        return give(k_four.at[owner[1]], kbuf.at[my_rows], owner, send_kv, recv_kv.at[1])
 
     def give_two(owner):
-        return give(kv_two.at[owner[1]], tbuf.at[my_rows], owner, send_kv, recv_kv.at[2, level])
-
-    q_rows = pl.ds(pl.multiple_of((me - half * (2 * blks // 2)) * rows, rows), rows)
+        return give(kv_two.at[owner[1]], tbuf.at[my_rows], owner, send_kv, recv_kv.at[2])
+
+    mine = me - half * blks
+    q_rows = pl.ds(pl.multiple_of(mine * rows, rows), rows)
 
     def give_q(owner):
         return give(q_all.at[owner[1]], qbuf.at[q_rows], owner, send_q, recv_q)
 
-    def others(h, body):
-        body((h, 1 - side))
-        mine = jnp.logical_and(uly == 1, blk == (half_levels - 1 + h) * 2 + side)
-        pl.when(jnp.logical_not(mine))(lambda: body((h, side)))
+    def across(h, *gives):
+        for one in gives:
+            one((h, 1 - side)).start()
+
+    def along(h, *gives):
+        here = jnp.logical_and(uly == 1, blk == (half_levels - 1 + h) * 2 + side)
+
+        @pl.when(jnp.logical_not(here))
+        def _():
+            for one in gives:
+                one((h, side)).start()
 
     def normalize(i, g):
         tiled = jnp.concatenate([gains[i]] * 4, axis=1)
@@ -405,35 +413,46 @@
         ).astype(jnp.bfloat16)
 
     loads[2].wait()
-    others(0, lambda o: give_v(o).start())
+    across(0, give_v)
     take(gains, gain_sem)
     loads[1].wait()
     for s in range(2):
         k_four[s] = normalize(1, 2 * s)
-    others(0, lambda o: give_k(o).start())
+    across(0, give_k)
+    along(0, give_v, give_k)
     middle = normalize(1, 1)
     for s in range(2):
         kv_two[s] = jnp.concatenate(
             [middle[:, s * pair:(s + 1) * pair], raw[2, :, wide + s * pair:wide + (s + 1) * pair]],
             axis=1,
         )
-    others(0, lambda o: give_two(o).start())
+    across(0, give_two)
+    along(0, give_two)
     loads[0].wait()
     middle = normalize(0, 1)
     pad = jnp.zeros((rows, 2 * LANES - pair), jnp.bfloat16)
     for s in range(2):
         q_all[s, :, 0:wide] = normalize(0, 2 * s)
         q_all[s, :, wide:] = jnp.concatenate([middle[:, s * pair:(s + 1) * pair], pad], axis=1)
-    pl.when(half == 0)(lambda: others(0, lambda o: give_q(o).start()))
+
+    @pl.when(half == 0)
+    def _():
+        across(0, give_q)
+        along(0, give_q)
 
     @pl.when(jnp.logical_not(late))
     def _():
         for i in range(2):
             pl.semaphore_wait(ready.at[i], 1)
 
-    for one in (give_v, give_k, give_two):
-        others(1, lambda o, one=one: one(o).start())
-    pl.when(half == 1)(lambda: others(1, lambda o: give_q(o).start()))
+    across(1, give_v, give_k, give_two)
+    along(1, give_v, give_k, give_two)
+
+    @pl.when(half == 1)
+    def _():
+        across(1, give_q)
+        along(1, give_q)
+
     give_w = pltpu.make_async_remote_copy(
         src_ref=w_hbm,
         dst_ref=w_vmem.at[my_depth],
@@ -453,14 +472,7 @@
         qbuf[q_rows, :] = q_all[side]
 
         def gathered(i, buf):
-            for l in range(levels):
-                @pl.when(l == level)
-                def _(l=l):
-                    take(buf.at[pl.ds(0, 3 * rows)], recv_kv.at[i, l])
-
-                @pl.when(l != level)
-                def _(l=l):
-                    take(buf.at[pl.ds(0, group)], recv_kv.at[i, l])
+            take(buf.at[pl.ds(0, buf.shape[0] - rows)], recv_kv.at[i])
 
         lane = lax.broadcasted_iota(jnp.int32, (part, 2 * LANES), 1)
 
@@ -488,20 +500,16 @@
             return jnp.where(first, weighted[:part], jnp.where(second, weighted[part:], 0.0))
 
         def send_back(src, dst, send, recv):
-            for i in range(part // rows):
-                b, c = half * (blks // 2) + i // 2, i % 2
-                home = jnp.logical_and(b == blk, uly == c)
-
-                @pl.when(jnp.logical_not(home))
-                def _(i=i, b=b, c=c):
-                    pltpu.make_async_remote_copy(
-                        src_ref=src.at[pl.ds(i * rows, rows)],
-                        dst_ref=dst.at[side],
-                        send_sem=send,
-                        recv_sem=recv.at[side],
-                        device_id={"blk": b, "uly": c},
-                        device_id_type=MESH,
-                    ).start()
+            for k in range(part // rows - 1):
+                i = k + (k >= mine).astype(jnp.int32)
+                pltpu.make_async_remote_copy(
+                    src_ref=src.at[pl.ds(pl.multiple_of(i * rows, rows), rows)],
+                    dst_ref=dst.at[side],
+                    send_sem=send,
+                    recv_sem=recv.at[side],
+                    device_id={"blk": half * (blks // 2) + i // 2, "uly": i % 2},
+                    device_id_type=MESH,
+                ).start()
 
             dst[side] = src[q_rows, :]
 
@@ -597,7 +605,7 @@
             pltpu.VMEM((width, cols), bf16),
             dma((3,)),
             dma, dma, dma, dma, dma, dma, dma,
-            dma((3, levels)),
+            dma((3,)),
             dma,
             dma((2,)),
             dma((2,)),

time: 13.4 us -> 13.4 us (level)
  no operation moved by 1% of the time
where the time goes in v4:
time: 13.4 us; the launch traced here: 13.2 us
  Pallas kernels  12.6 us (94%)
  local copies, waits for them, and re-layouts  0.64 us (5%)
    pallas_call x1, Pallas kernels, on_device_gather(): pl.pallas_call(functools.partial(gather_kernel, blks, heads), out_shape=p...  12.6 us
    unnamed x1, local copies, waits for them, and re-layouts  0.64 us

profile of v4, /device:TPU:0, one launch (start us, length us, event | category | flops | bytes accessed | tf_op | source)
XLA Modules:
  0.0 13.2 jit_solution(11009747431362753776)
XLA Ops:
  0.0 12.6 %shard_map.64 = bf16[16,2304]{1,0:T(8,128)(2,1)S(1)} custom-call(bf16[16,1152]{1,0:T(8,128)(2,1)} %q_hbm.1, bf16[16,1152]{1,0:T(8,128)(2,1)} %k_hbm.1, bf16[16,1152]{1,0:T(8,128)(2,1)} %v_hbm.1, f32[1,96]{1,0:T(1,128)} %bitcast.2, f32[1,96]{1,0:T(1,128)} %bitcast.3, bf16[576,2304]{1,0:T(8,128)(2,1)} %w_hbm.1), custom_call_target="tpu_custom_call" | custom-call | tf_op jit(solution)/shard_map/pallas_call | solution.py:585
  12.6 0.6 %copy.8 = bf16[16,2304]{1,0:T(8,128)(2,1)} copy(bf16[16,2304]{1,0:T(8,128)(2,1)S(1)} %shard_map.64) | data formatting | bytes 147456

commit v5 on v4

--- a/solution.py
+++ b/solution.py
@@ -413,21 +413,25 @@
         ).astype(jnp.bfloat16)
 
     loads[2].wait()
+    straight = jnp.logical_and(level > half_levels, side == 0)
+    pl.when(straight)(lambda: along(0, give_v))
     across(0, give_v)
     take(gains, gain_sem)
     loads[1].wait()
     for s in range(2):
         k_four[s] = normalize(1, 2 * s)
+    pl.when(straight)(lambda: along(0, give_k))
     across(0, give_k)
-    along(0, give_v, give_k)
+    pl.when(jnp.logical_not(straight))(lambda: along(0, give_v, give_k))
     middle = normalize(1, 1)
     for s in range(2):
         kv_two[s] = jnp.concatenate(
             [middle[:, s * pair:(s + 1) * pair], raw[2, :, wide + s * pair:wide + (s + 1) * pair]],
             axis=1,
         )
+    pl.when(straight)(lambda: along(0, give_two))
     across(0, give_two)
-    along(0, give_two)
+    pl.when(jnp.logical_not(straight))(lambda: along(0, give_two))
     loads[0].wait()
     middle = normalize(0, 1)
     pad = jnp.zeros((rows, 2 * LANES - pair), jnp.bfloat16)
@@ -553,24 +557,22 @@
     acc[...] = project4(side, True)
     acc[...] += project4(1 - side, False)
     acc[...] += project2(side, True)
-    out_ref[...] = (acc[...] + project2(1 - side, False)).astype(out_ref.dtype)
 
     give_w.wait_send()
     slab = tbuf.at[pl.ds(0, rows)]
     for i in range(9):
         take(slab, send_kv)
     take(qbuf.at[pl.ds(0, rows)], send_q)
-
-    @pl.when(is_owner)
-    def _():
-        take(four.at[pl.ds(0, part - rows)], send4)
-        take(two.at[pl.ds(0, part - rows)], send2)
+    pl.when(is_owner)(lambda: take(four.at[pl.ds(0, part - rows)], send4))
 
     @pl.when(jnp.logical_not(is_owner))
     def _():
         for i in range(3):
             take(slab, send_kv)
         take(qbuf.at[pl.ds(0, rows)], send_q)
+
+    out_ref[...] = (acc[...] + project2(1 - side, False)).astype(out_ref.dtype)
+    pl.when(is_owner)(lambda: take(two.at[pl.ds(0, part - rows)], send2))
 
 
 def on_device_gather(blks, query, key, value, q_gain, k_gain, out_weight):

time: 13.4 us -> 13.3 us (level)
  no operation moved by 1% of the time
where the time goes in v5:
time: 13.3 us; the launch traced here: 13.2 us
  Pallas kernels  12.5 us (94%)
  local copies, waits for them, and re-layouts  0.64 us (5%)
    pallas_call x1, Pallas kernels, on_device_gather(): pl.pallas_call(functools.partial(gather_kernel, blks, heads), out_shape=p...  12.5 us
    unnamed x1, local copies, waits for them, and re-layouts  0.64 us

profile of v5, /device:TPU:0, one launch (start us, length us, event | category | flops | bytes accessed | tf_op | source)
XLA Modules:
  0.0 13.2 jit_solution(14667180264652357425)
XLA Ops:
  0.0 12.5 %shard_map.64 = bf16[16,2304]{1,0:T(8,128)(2,1)S(1)} custom-call(bf16[16,1152]{1,0:T(8,128)(2,1)} %q_hbm.1, bf16[16,1152]{1,0:T(8,128)(2,1)} %k_hbm.1, bf16[16,1152]{1,0:T(8,128)(2,1)} %v_hbm.1, f32[1,96]{1,0:T(1,128)} %bitcast.2, f32[1,96]{1,0:T(1,128)} %bitcast.3, bf16[576,2304]{1,0:T(8,128)(2,1)} %w_hbm.1), custom_call_target="tpu_custom_call" | custom-call | tf_op jit(solution)/shard_map/pallas_call | solution.py:587
  12.5 0.6 %copy.8 = bf16[16,2304]{1,0:T(8,128)(2,1)} copy(bf16[16,2304]{1,0:T(8,128)(2,1)S(1)} %shard_map.64) | data formatting | bytes 147456

commit v6 on v5

--- a/solution.py
+++ b/solution.py
@@ -273,7 +273,7 @@
 def gather_kernel(
     blks, heads,
     q_hbm, k_hbm, v_hbm, qg_hbm, kg_hbm, w_hbm, out_ref,
-    raw, gains, k_four, kv_two, q_all, kbuf, vbuf, tbuf, qbuf, four, two, back4, back2, acc, w_vmem,
+    raw, gains, k_four, kv_two, q_all, kbuf, vbuf, tbuf, qbuf, four, two, back4, back2, acc, w_vmem, stacked,
     load_sem, gain_sem, w_sem, send_kv, send_q, send4, send2, send_w,
     recv_kv, recv_q, recv4, recv2, recv_w, ready,
 ):
@@ -486,14 +486,16 @@
                 jnp.logical_and(lane >= off + HD, lane < off + 2 * HD),
             )
 
-        def attend(query, off, keys, values, value_off):
+        def stack(j, query, off):
             first, second = heads_at(off)
             zero = jnp.zeros_like(query)
-            query = jnp.concatenate(
+            stacked[j] = jnp.concatenate(
                 [jnp.where(first, query, zero), jnp.where(second, query, zero)], axis=0
             )
+
+        def attend(j, keys, values, value_off):
             scores = lax.dot_general(
-                query, keys, (((1,), (1,)), ((), ())), preferred_element_type=jnp.float32
+                stacked[j], keys, (((1,), (1,)), ((), ())), preferred_element_type=jnp.float32
             )
             expd = jnp.exp2(scores * (float(HD) ** (-0.5) * LOG2E))
             total = jnp.sum(expd, axis=-1, keepdims=True)
@@ -518,11 +520,14 @@
             dst[side] = src[q_rows, :]
 
         take(qbuf.at[pl.ds(0, part - rows)], recv_q)
+        stack(0, qbuf[:, 0:2 * LANES], 0)
+        stack(1, qbuf[:, LANES:wide], pair - LANES)
+        stack(2, qbuf[:, wide:], 0)
         gathered(0, vbuf)
         gathered(1, kbuf)
-        low = attend(qbuf[:, 0:2 * LANES], 0, kbuf[:, 0:2 * LANES], vbuf[:, 0:2 * LANES], 0)
+        low = attend(0, kbuf[:, 0:2 * LANES], vbuf[:, 0:2 * LANES], 0)
         high = attend(
-            qbuf[:, LANES:wide], pair - LANES, kbuf[:, LANES:wide], vbuf[:, LANES:wide], pair - LANES
+            1, kbuf[:, LANES:wide], vbuf[:, LANES:wide], pair - LANES
         )
         four[...] = jnp.concatenate(
             [low[:, :LANES], low[:, LANES:] + high[:, :LANES], high[:, LANES:]], axis=1
@@ -530,7 +535,7 @@
         send_back(four, back4, send4, recv4)
         gathered(2, tbuf)
         two[...] = attend(
-            qbuf[:, wide:], 0, tbuf[:, 0:2 * LANES], tbuf[:, LANES:], pair - LANES
+            2, tbuf[:, 0:2 * LANES], tbuf[:, LANES:], pair - LANES
         ).astype(jnp.bfloat16)
         send_back(two, back2, send2, recv2)
 
@@ -605,6 +610,7 @@
             pltpu.VMEM((2, rows, two), bf16),
             pltpu.VMEM((rows, cols), jnp.float32),
             pltpu.VMEM((width, cols), bf16),
+            pltpu.VMEM((3, seq, two), bf16),
             dma((3,)),
             dma, dma, dma, dma, dma, dma, dma,
             dma((3,)),

time: 13.3 us -> 13.3 us (level)
  no operation moved by 1% of the time
where the time goes in v6:
time: 13.3 us; the launch traced here: 13.2 us
  Pallas kernels  12.5 us (94%)
  local copies, waits for them, and re-layouts  0.64 us (5%)
    pallas_call x1, Pallas kernels, on_device_gather(): pl.pallas_call(functools.partial(gather_kernel, blks, heads), out_shape=p...  12.5 us
    unnamed x1, local copies, waits for them, and re-layouts  0.64 us

profile of v6, /device:TPU:0, one launch (start us, length us, event | category | flops | bytes accessed | tf_op | source)
XLA Modules:
  0.0 13.2 jit_solution(11975731407668247880)
XLA Ops:
  0.0 12.5 %shard_map.64 = bf16[16,2304]{1,0:T(8,128)(2,1)S(1)} custom-call(bf16[16,1152]{1,0:T(8,128)(2,1)} %q_hbm.1, bf16[16,1152]{1,0:T(8,128)(2,1)} %k_hbm.1, bf16[16,1152]{1,0:T(8,128)(2,1)} %v_hbm.1, f32[1,96]{1,0:T(1,128)} %bitcast.2, f32[1,96]{1,0:T(1,128)} %bitcast.3, bf16[576,2304]{1,0:T(8,128)(2,1)} %w_hbm.1), custom_call_target="tpu_custom_call" | custom-call | tf_op jit(solution)/shard_map/pallas_call | solution.py:592
  12.6 0.6 %copy.8 = bf16[16,2304]{1,0:T(8,128)(2,1)} copy(bf16[16,2304]{1,0:T(8,128)(2,1)S(1)} %shard_map.64) | data formatting | bytes 147456
